TPU v7x, 32 devices: a whole 2x2x4 slice. The times are simulated.
32 devices in a mesh: col: 4 (over y, x), row: 8 (over z, core).
Axes of the slice: x: 2, y: 2, z: 4, core: 2. Of those that a mesh axis runs over, the one named last changes fastest.
Arguments:
- object_field: float32 [2, 4096, 2048], P(None, 'row', 'col'), may hold values from -20 to 20
- probe_field: float32 [2, 256, 256], replicated, may hold values from -4.2 to 4.2
- amplitudes: float32 [8, 4, 2, 256, 256], P('row', 'col'), may hold values from 0.25 to 2.5
- positions: int32 [8, 4, 2, 2], P('row', 'col'), may hold values from -128 to 384, as said below
- batch_order: int32 [8, 4, 2], P('row', 'col'), may hold values from 0 to 1, each once within a row
Outputs:
- object_out: float32 [2, 4096, 2048], P(None, 'row', 'col')
- probe_out: float32 [2, 256, 256], replicated
Inputs may be any that keep to these rules, and one draw needn't show every extreme that they name: `positions`: in every tile some pattern's window reaches past its upper edge, some past its lower edge, some past its left edge and some past its right edge. `batch_order`: each tile's 2 entries name each of its patterns once.
All inputs are finite; a program needn't handle non-finite values.
Results may differ from a plain program's by a relative error of at most 0.0065.
Values sent between devices are 32-bit elements; how exact they have to be, the bound alone decides.
A program may use at most 128 MiB of HBM per device.

v0:
```python
import functools
import math

import jax
import jax.numpy as jnp
import numpy as np
from jax import lax
from jax.experimental import pallas as pl
from jax.experimental.pallas import tpu as pltpu
from jax.sharding import PartitionSpec as P

OV = 128

ALPHA = 0.5
BETA = 4.0
FLOOR = 0.5
EPSILON = 1e-06

UP, DOWN, LEFT, RIGHT = 0, 1, 2, 3
CHUNKS = 4


def dft_tables(size_w):
    counter = np.arange(size_w)
    angles = 2.0 * math.pi / size_w * (counter[:, None] * counter[None, :] % size_w)
    both = np.concatenate([np.cos(angles), np.sin(angles)], axis=1) / math.sqrt(size_w)
    both = both.astype(np.float32)
    head = both.astype(jnp.bfloat16)
    rest = (both - head.astype(np.float32)).astype(jnp.bfloat16)
    return head, rest


def halves(value):
    head = value.astype(jnp.bfloat16)
    rest = (value - head.astype(jnp.float32)).astype(jnp.bfloat16)
    return head, rest


def dot(left, right):
    return jnp.dot(left, right, preferred_element_type=jnp.float32)


def left_apply(tab_head, tab_rest, re_part, im_part, sign):
    size = re_part.shape[0]
    head, rest = halves(jnp.concatenate([re_part, im_part], axis=1))
    out = dot(tab_head, head) + dot(tab_head, rest) + dot(tab_rest, head)
    cos_re, cos_im = out[:size, :size], out[:size, size:]
    sin_re, sin_im = out[size:, :size], out[size:, size:]
    return cos_re + sign * sin_im, cos_im - sign * sin_re


def right_apply(re_part, im_part, tab_head, tab_rest, sign):
    size = re_part.shape[0]
    head, rest = halves(jnp.concatenate([re_part, im_part], axis=0))
    out = dot(head, tab_head) + dot(rest, tab_head) + dot(head, tab_rest)
    re_cos, re_sin = out[:size, :size], out[:size, size:]
    im_cos, im_sin = out[size:, :size], out[size:, size:]
    return re_cos + sign * im_sin, im_cos - sign * re_sin


def pick(flag, first, second):
    return jnp.where(flag == 1, first, second)


def keep(flag, value):
    return jnp.where(flag == 1, value, 0.0)


def across(*parts):
    return jnp.concatenate(parts, axis=1)


def stacked(*parts):
    return jnp.concatenate(parts, axis=0)


class Spot:
    def __init__(self, row, col, tile):
        half = tile // 2
        inside = lambda place: jnp.where(
            place < 0, jnp.maximum(place, -OV), jnp.clip(place, half, half + OV)
        )
        row, col = inside(row), inside(col)
        self.row, self.col = row, col
        self.up = jnp.where(row < 0, 1, 0)
        self.left = jnp.where(col < 0, 1, 0)
        self.row_on = jnp.where(row < 0, row + OV, row - half)
        self.col_on = jnp.where(col < 0, col + OV, col - half)


def choose(flag, first, second, tile):
    return Spot(
        jnp.where(flag == 1, first.row, second.row),
        jnp.where(flag == 1, first.col, second.col),
        tile,
    )


def same(first, second):
    return 1 - (first - second) * (first - second)


def kernel(
    rows, cols, pos, order, obj, probe_in, amps_in, lh_in, lr_in, rh_in, rr_in,
    out, probe_out,
    own, rim, mid, probe, amps, lh, lr, rh, rr, info, infos, hs, hr, vbuf, placed,
    bs, br, bnd_s, bnd_r, dreg, cs, cr, mid_s, mid_r, rim_s, rim_r,
    psum, acc, rx0, rx1, red, rx2, res, pw, pw0, pwa, pw1, pw2,
    local_sems, send_sems, recv_sems,
):
    tile = own.shape[2]
    blocks = tile // OV
    size_w = probe.shape[-1]
    half = tile // 2
    span = half + OV
    row, col = lax.axis_index("row"), lax.axis_index("col")
    core, par = row % 2, col % 2
    at = lambda r, c: {"row": r, "col": c}
    above, below = at((row + rows - 1) % rows, col), at((row + 1) % rows, col)
    west, east = at(row, (col + cols - 1) % cols), at(row, (col + 1) % cols)
    partner = at(row, col + 1 - 2 * par)
    onward = at(row, (col + 2 - 4 * par + cols) % cols)
    sibling = at(row + 1 - 2 * core, col)
    used = [0, 0]

    def fetch(source, target):
        copy = pltpu.make_async_copy(source, target, local_sems.at[used[0]])
        used[0] += 1
        copy.start()
        return copy

    def send(source, target, device):
        copy = pltpu.make_async_remote_copy(
            src_ref=source,
            dst_ref=target,
            send_sem=send_sems.at[used[1]],
            recv_sem=recv_sems.at[used[1]],
            device_id=device,
            device_id_type=pl.DeviceIdType.MESH,
        )
        used[1] += 1
        copy.start()
        sent.append(copy)
        return copy

    sent = []
    lanes = [pl.ds(block * OV, OV) for block in range(blocks)]
    own_in = [fetch(obj.at[:, :, lanes[block]], own.at[:, block]) for block in range(blocks)]
    rim_in = [
        fetch(obj.at[:, :, lanes[block]], rim.at[side, :, pl.ds(OV, tile), :])
        for side, block in ((0, 0), (1, blocks - 1))
    ]
    tall_in = [
        fetch(obj.at[:, :, lanes[block]], mid.at[block - 1, :, pl.ds(OV, tile), :])
        for block in range(1, blocks - 1)
    ]
    rest_in = [
        fetch(source, target)
        for source, target in (
            (probe_in, probe), (lh_in, lh), (lr_in, lr), (rh_in, rh), (rr_in, rr), (amps_in, amps),
        )
    ]

    mine = []
    for batch in range(2):
        which = order[batch]
        info[2 * batch] = pos[0, which]
        info[2 * batch + 1] = pos[1, which]
        mine.append(Spot(pos[0, which], pos[1, which], tile))

    barrier = pltpu.get_barrier_semaphore()
    peers = [above, below]
    peers += [at(row, (col + d) % cols) for d in range(1, cols)]
    peers += [at((row + 2 * d) % rows, col) for d in range(1, rows // 2)]
    for peer in peers:
        pl.semaphore_signal(barrier, inc=1, device_id=peer, device_id_type=pl.DeviceIdType.MESH)
    pl.semaphore_wait(barrier, len(peers))

    info_in = {}
    for peer, slot in ((west, RIGHT), (east, LEFT), (above, DOWN), (below, UP)):
        info_in[slot] = send(info, infos.at[slot], peer)
    side_block = (0, blocks - 1)
    edge_in, mid_in = [], []

    def send_past(block, tall):
        return [
            send(obj.at[:, pl.ds(0, OV), lanes[block]], tall.at[:, pl.ds(OV + tile, OV), :], above),
            send(obj.at[:, pl.ds(tile - OV, OV), lanes[block]], tall.at[:, pl.ds(0, OV), :], below),
        ]

    for side in range(2):
        edge_in += send_past(side_block[side], rim.at[side])
    for block in range(1, blocks - 1):
        mid_in += send_past(block, mid.at[block - 1])

    for copy in own_in:
        copy.wait()
    for index in range(4):
        for block in range(span // OV):
            gap = jnp.zeros((OV, OV), jnp.float32)
            placed[index, block, pl.ds(0, OV), :] = gap
            placed[index, block, pl.ds(OV + size_w, OV), :] = gap

    near = {}

    def spots(slot):
        info_in[slot].wait_recv()
        near[slot] = [Spot(infos[slot, 2 * b], infos[slot, 2 * b + 1], tile) for b in range(2)]

    spots(LEFT)
    spots(RIGHT)
    west_first = 1 - near[LEFT][0].left
    east_first = near[RIGHT][0].left
    west_spot = choose(west_first, near[LEFT][0], near[LEFT][1], tile)
    east_spot = choose(east_first, near[RIGHT][0], near[RIGHT][1], tile)
    wanted = (west_spot, east_spot)

    halo_in = {}
    for side in range(2):
        spot = wanted[side]
        start = jnp.where(spot.up == 1, spot.row + OV, spot.row)
        for part in range(2):
            hs[side, 0, part] = own[part, side_block[side], pl.ds(start, OV), :]
        halo_in[1 - side, 0] = send(
            hs.at[side, 0], hr.at[1 - side, 0], (west, east)[side]
        )

    squares = jnp.zeros((8, OV), jnp.float32)
    for part in range(2):
        for block in range(blocks):
            value = own[part, block]
            squares = squares + jnp.sum((value * value).reshape(tile // 8, 8, OV), axis=0)
    pw[...] = squares

    for copy in edge_in:
        copy.wait_recv()
    for copy in rim_in:
        copy.wait()
    for side in range(2):
        spot = wanted[side]
        start = jnp.where(spot.up == 1, spot.row + OV, spot.row + 2 * OV)
        for part in range(2):
            hs[side, 1, part] = rim[side, part, pl.ds(start, OV), :]
        halo_in[1 - side, 1] = send(
            hs.at[side, 1], hr.at[1 - side, 1], (west, east)[side]
        )

    for copy in mid_in:
        copy.wait_recv()
    for copy in tall_in:
        copy.wait()
    for copy in rest_in:
        copy.wait()
    spots(UP)
    spots(DOWN)
    power_probe = jnp.sum(
        probe[0] * probe[0] + probe[1] * probe[1], axis=(0, 1), keepdims=True
    )
    step_object = ALPHA / (power_probe / float(size_w * size_w) + EPSILON)

    def cut(value, spot):
        back = jnp.where(spot.col_on == 0, 0, span - spot.col_on)
        return pltpu.roll(value, back, 1)[:, :size_w]

    for copy in halo_in.values():
        copy.wait_recv()
    for batch in range(2):
        spot = mine[batch]
        for part in range(2):
            first = pick(spot.left, hr[0, 0, part], hr[1, 0, part])
            second = pick(spot.left, hr[0, 1, part], hr[1, 1, part])
            strip = pick(spot.up, stacked(second, first), stacked(first, second))
            window = pl.ds(spot.row + OV, size_w)
            tall = [rim[0, part, window, :]]
            tall += [mid[block - 1, part, window, :] for block in range(1, blocks - 1)]
            tall.append(rim[1, part, window, :])
            near_half = half // OV
            body = pick(spot.left, across(*tall[:near_half]), across(*tall[near_half:]))
            region = pick(spot.left, across(strip, body), across(body, strip))
            vbuf[2 * batch + part] = cut(region, spot)

    def transform(batch):
        spot = mine[batch]
        win_re, win_im = vbuf[2 * batch], vbuf[2 * batch + 1]
        probe_re, probe_im = probe[0], probe[1]
        exit_re = probe_re * win_re - probe_im * win_im
        exit_im = probe_re * win_im + probe_im * win_re
        half_re, half_im = left_apply(lh[...], lr[...], exit_re, exit_im, 1.0)
        far_re, far_im = right_apply(half_re, half_im, rh[...], rr[...], 1.0)
        modulus = jnp.sqrt(far_re * far_re + far_im * far_im)
        scaled = amps[order[batch]] / jnp.maximum(modulus, FLOOR)
        half_re, half_im = left_apply(
            lh[...], lr[...], far_re - scaled * far_re, far_im - scaled * far_im, -1.0
        )
        back_re, back_im = right_apply(half_re, half_im, rh[...], rr[...], -1.0)
        terms = (
            win_re * back_re + win_im * back_im,
            win_re * back_im - win_im * back_re,
        )
        for part in range(2):
            psum[part] = terms[part] if batch == 0 else psum[part] + terms[part]
        moves = (
            probe_re * back_re + probe_im * back_im,
            probe_re * back_im - probe_im * back_re,
        )
        beside = jnp.zeros((size_w, span - size_w), jnp.float32)
        for part in range(2):
            wide = across(step_object * moves[part], beside)
            wide = pltpu.roll(wide, spot.col_on, 1)
            for block in range(span // OV):
                placed[2 * batch + part, block, pl.ds(OV, size_w), :] = wide[:, block * OV : (block + 1) * OV]

    def load_placed(index, start, count):
        rows_of = pl.ds(start, count)
        return across(*[placed[index, block, rows_of, :] for block in range(span // OV)])

    def frame(batch, part, kind):
        spot = mine[batch]
        upper, lower = {"past": (-OV, tile), "edge": (0, tile - OV), "deep": (OV, half)}[kind]
        start = OV - spot.row + jnp.where(spot.up == 1, upper, lower)
        return load_placed(2 * batch + part, start, OV)

    transform(0)

    split = 2 * OV // CHUNKS
    per = OV // split
    block_in, block_on = [], []
    spot = mine[0]
    for chunk in range(CHUNKS):
        kind = ("edge", "deep")[chunk // per]
        low = (chunk % per) * split
        for part in range(2):
            value = frame(0, part, kind)[low : low + split]
            bs[chunk, part] = pick(spot.left, value[:, : 2 * OV], value[:, span - 2 * OV :])
        block_in.append(send(bs.at[chunk], br.at[par, chunk], partner))

    def hand_on(copy, buffer, index):
        copy.wait_recv()
        return send(buffer.at[1 - par, index], buffer.at[par, index], onward)

    for part in range(2):
        value = frame(0, part, "past")
        cs[0, part] = pick(spot.left, value[:, :OV], value[:, span - OV :])
    for chunk in range(per):
        block_on.append(hand_on(block_in[chunk], br, chunk))
    corner_in = [send(cs.at[0], cr.at[par, 0], partner)]
    for copy in block_on:
        copy.wait_recv()

    def near_block(side, part, kind):
        base = 0 if kind == "edge" else per
        return stacked(*[br[side, base + k, part] for k in range(per)])

    toward = (1 - near[LEFT][0].left, near[RIGHT][0].left)
    blank = jnp.zeros((OV, span - 2 * OV), jnp.float32)
    band_in = []
    for way, slot in ((0, UP), (1, DOWN)):
        goal = near[slot][1]
        match = spot.up if way == 0 else 1 - spot.up
        use_own = match * same(spot.left, goal.left)
        ups = [near[LEFT][0].up, near[RIGHT][0].up]
        if way == 1:
            ups = [1 - flag for flag in ups]
        use = jnp.where(goal.left == 1, ups[0] * toward[0], ups[1] * toward[1])
        for part in range(2):
            block = pick(goal.left, near_block(0, part, "edge"), near_block(1, part, "edge"))
            block = keep(use, block)
            whole = keep(use_own, frame(0, part, "edge"))
            whole = whole + pick(goal.left, across(block, blank), across(blank, block))
            bnd_s[way, part] = cut(whole, goal)
        band_in.append(
            send(bnd_s.at[way], bnd_r.at[1 - way], (above, below)[way])
        )
    for chunk in range(per, CHUNKS):
        block_on.append(hand_on(block_in[chunk], br, chunk))
    corner_on = [hand_on(corner_in[0], cr, 0)]
    for copy in block_on[per:]:
        copy.wait_recv()

    spot = mine[1]
    use = jnp.where(
        spot.left == 1,
        toward[0] * same(near[LEFT][0].up, spot.up),
        toward[1] * same(near[RIGHT][0].up, spot.up),
    )
    wide_blank = jnp.zeros((half, span - 2 * OV), jnp.float32)
    inside = []
    for part in range(2):
        at_edge = pick(spot.left, near_block(0, part, "edge"), near_block(1, part, "edge"))
        deep = pick(spot.left, near_block(0, part, "deep"), near_block(1, part, "deep"))
        block = keep(use, pick(spot.up, stacked(at_edge, deep), stacked(deep, at_edge)))
        inside.append(cut(pick(spot.left, across(block, wide_blank), across(wide_blank, block)), spot))
    for copy in band_in:
        copy.wait_recv()
    for part in range(2):
        band = pick(spot.up, bnd_r[0, part], bnd_r[1, part])
        region = pick(spot.up, stacked(band, inside[part]), stacked(inside[part], band))
        for block in range(size_w // OV):
            dreg[part, block] = region[:, block * OV : (block + 1) * OV]
    for part in range(2):
        change = [dreg[part, b, pl.ds(spot.row_on, size_w), :] for b in range(size_w // OV)]
        vbuf[2 + part] = vbuf[2 + part] - across(*change)

    transform(1)

    pair_in = send(psum.at[1 - core], rx0, sibling)
    power_in = [send(pw, pw0, sibling)]

    for index, kind in ((1, "past"), (2, "edge"), (3, "deep")):
        for part in range(2):
            value = frame(1, part, kind)
            cs[index, part] = pick(spot.left, value[:, :OV], value[:, span - OV :])
    pair_in.wait_recv()
    acc[...] = psum[core] + rx0[...]
    power_in[0].wait_recv()
    pwa[...] = pw[...] + pw0[...]
    piece = size_w // cols
    part_in = []
    for step in range(1, cols):
        other = (col + step) % cols
        part_in.append(
            send(acc.at[pl.ds(other * piece, piece)], rx1.at[step - 1], at(row, other))
        )
        power_in.append(send(pwa, pw1.at[col], at(row, other)))
    for index in range(1, 4):
        corner_in.append(send(cs.at[index], cr.at[par, index], partner))

    first_up = mine[0].up
    out_spots = (
        choose(first_up, mine[0], mine[1], tile),
        choose(first_up, mine[1], mine[0], tile),
    )
    out_batch = (1 - first_up, first_up)
    up_start = jnp.maximum(OV - out_spots[0].row, OV)

    def wide_own(way, part, start, count):
        value = load_placed(2 * out_batch[way] + part, start, count)
        left = out_spots[way].left
        body = pick(left, value[:, OV:], value[:, :half])
        gap = jnp.zeros((count, half), jnp.float32)
        return pick(left, across(body, gap), across(gap, body))

    past_in = []
    for way in range(2):
        start = up_start - OV if way == 0 else OV + tile - out_spots[1].row
        for part in range(2):
            value = wide_own(way, part, start, OV)
            mid_s[way, part] = value[:, OV : tile - OV]
            rim_s[way, 0, part] = value[:, :OV]
            rim_s[way, 1, part] = value[:, tile - OV :]

    mine_piece = acc[pl.ds(pl.multiple_of(col * piece, piece), piece), :]
    for copy in part_in:
        copy.wait_recv()
    for step in range(cols - 1):
        mine_piece = mine_piece + rx1[step]
    red[...] = mine_piece
    for copy in power_in[1:]:
        copy.wait_recv()
    pw1[col] = pwa[...]
    total = pw1[0]
    for place in range(1, cols):
        total = total + pw1[place]
    pw2[rows // 2] = total
    plane = row // 2
    plane_in = []
    for step in range(1, rows // 2):
        goal = at((row + 2 * step) % rows, col)
        plane_in.append(send(red, rx2.at[plane], goal))
        plane_in.append(send(pw2.at[rows // 2], pw2.at[plane], goal))
    for way in range(2):
        past_in.append(send(mid_s.at[way], mid_r.at[1 - way], (above, below)[way]))

    corner_on.append(hand_on(corner_in[1], cr, 1))
    corner_on.append(hand_on(corner_in[2], cr, 2))
    corner_on.append(hand_on(corner_in[3], cr, 3))

    for copy in plane_in:
        copy.wait_recv()
    rx2[plane] = red[...]
    pw2[plane] = total
    whole, total = rx2[0], pw2[0]
    for place in range(1, rows // 2):
        whole = whole + rx2[place]
        total = total + pw2[place]
    here = pl.ds(pl.multiple_of(col * piece, piece), piece)
    res[core, here, :] = whole
    gather_in = []
    for step in range(1, cols):
        other = at(row, (col + step) % cols)
        gather_in.append(send(res.at[core, here], res.at[core, here], other))

    corner_on[0].wait_recv()
    corner_on[1].wait_recv()
    for way in range(2):
        for side in range(2):
            theirs = wanted[side]
            first = (west_first, east_first)[side]
            match = theirs.up if way == 0 else 1 - theirs.up
            for part in range(2):
                corner = pick(first, cr[side, 0, part], cr[side, 1, part])
                rim_s[way, side, part] = rim_s[way, side, part] + keep(match, corner)
    for way in range(2):
        past_in.append(send(rim_s.at[way], rim_r.at[1 - way], (above, below)[way]))

    for copy in gather_in:
        copy.wait_recv()
    last_in = send(res.at[core], res.at[core], sibling)

    corner_on[2].wait_recv()
    corner_on[3].wait_recv()
    for copy in past_in:
        copy.wait_recv()
    gap = jnp.zeros((half, tile - 2 * OV), jnp.float32)
    for part in range(2):
        outer = []
        for side in range(2):
            first = (west_first, east_first)[side]
            part_of = slice(OV, 2 * OV) if side == 0 else slice(0, OV)
            at_edge = pick(first, near_block(side, part, "edge")[:, part_of], cr[side, 2, part])
            deep = pick(first, near_block(side, part, "deep")[:, part_of], cr[side, 3, part])
            up = wanted[side].up
            outer.append((up, at_edge, deep))
        for way in range(2):
            start = up_start if way == 0 else OV + half - out_spots[1].row
            value = wide_own(way, part, start, half)
            strips = []
            for up, at_edge, deep in outer:
                flag = up if way == 0 else 1 - up
                strips.append(
                    keep(flag, stacked(at_edge, deep) if way == 0 else stacked(deep, at_edge))
                )
            value = value + across(strips[0], gap, strips[1])
            late = across(rim_r[way, 0, part], mid_r[way, part], rim_r[way, 1, part])
            rest = jnp.zeros((half - OV, tile), jnp.float32)
            value = value + (stacked(late, rest) if way == 0 else stacked(rest, late))
            band = pl.ds(way * half, half)
            old = across(*[own[part, block, band, :] for block in range(blocks)])
            out[part, band, :] = old - value

    last_in.wait_recv()
    cell_count = float(tile * tile * rows * cols)
    mean_power = jnp.sum(total, axis=(0, 1), keepdims=True) / cell_count + EPSILON
    step_probe = BETA * size_w * size_w / (cell_count * mean_power)
    for part in range(2):
        probe_out[part] = probe[part] - step_probe * res[part]
    for copy in sent:
        copy.wait_send()


def local(mesh_shape, object_field, probe_field, amplitudes, positions, batch_order):
    rows, cols = mesh_shape["row"], mesh_shape["col"]
    size_w = probe_field.shape[-1]
    tile = object_field.shape[1]
    half = tile // 2
    span = half + OV
    head, rest = dft_tables(size_w)
    f32 = lambda *shape: pltpu.VMEM(shape, jnp.float32)
    b16 = lambda *shape: pltpu.VMEM(shape, jnp.bfloat16)
    piece = size_w // cols
    split = 2 * OV // CHUNKS
    scratch = dict(
        own=f32(2, tile // OV, tile, OV),
        rim=f32(2, 2, tile + 2 * OV, OV),
        mid=f32(tile // OV - 2, 2, tile + 2 * OV, OV),
        probe=f32(2, size_w, size_w),
        amps=f32(2, size_w, size_w),
        lh=b16(2 * size_w, size_w),
        lr=b16(2 * size_w, size_w),
        rh=b16(size_w, 2 * size_w),
        rr=b16(size_w, 2 * size_w),
        info=pltpu.SMEM((4,), jnp.int32),
        infos=pltpu.SMEM((4, 4), jnp.int32),
        hs=f32(2, 2, 2, OV, OV),
        hr=f32(2, 2, 2, OV, OV),
        vbuf=f32(4, size_w, size_w),
        placed=f32(4, span // OV, size_w + 2 * OV, OV),
        bs=f32(CHUNKS, 2, split, 2 * OV),
        br=f32(2, CHUNKS, 2, split, 2 * OV),
        bnd_s=f32(2, 2, OV, size_w),
        bnd_r=f32(2, 2, OV, size_w),
        dreg=f32(2, size_w // OV, span, OV),
        cs=f32(4, 2, OV, OV),
        cr=f32(2, 4, 2, OV, OV),
        mid_s=f32(2, 2, OV, tile - 2 * OV),
        mid_r=f32(2, 2, OV, tile - 2 * OV),
        rim_s=f32(2, 2, 2, OV, OV),
        rim_r=f32(2, 2, 2, OV, OV),
        psum=f32(2, size_w, size_w),
        acc=f32(size_w, size_w),
        rx0=f32(size_w, size_w),
        rx1=f32(cols - 1, piece, size_w),
        red=f32(piece, size_w),
        rx2=f32(rows // 2, piece, size_w),
        res=f32(2, size_w, size_w),
        pw=f32(8, 128),
        pw0=f32(8, 128),
        pwa=f32(8, 128),
        pw1=f32(cols, 8, 128),
        pw2=f32(rows // 2 + 1, 8, 128),
    )
    sends = 96 + 4 * cols + 2 * rows
    hbm = pl.BlockSpec(memory_space=pl.ANY)
    vmem = pl.BlockSpec(memory_space=pltpu.VMEM)
    smem = pl.BlockSpec(memory_space=pltpu.SMEM)
    dma = pltpu.SemaphoreType.DMA
    return pl.pallas_call(
        functools.partial(kernel, rows, cols),
        out_shape=(
            jax.ShapeDtypeStruct(object_field.shape, jnp.float32),
            jax.ShapeDtypeStruct(probe_field.shape, jnp.float32),
        ),
        in_specs=[smem, smem] + [hbm] * 7,
        out_specs=(vmem, vmem),
        scratch_shapes=list(scratch.values()) + [dma((32,)), dma((sends,)), dma((sends,))],
        compiler_params=pltpu.CompilerParams(
            collective_id=0, has_side_effects=True, vmem_limit_bytes=56 * 1024 * 1024
        ),
    )(
        positions[0, 0],
        batch_order[0, 0],
        object_field,
        probe_field,
        amplitudes[0, 0],
        jnp.asarray(np.concatenate(np.split(head, 2, axis=1), axis=0)),
        jnp.asarray(np.concatenate(np.split(rest, 2, axis=1), axis=0)),
        jnp.asarray(head),
        jnp.asarray(rest),
    )


def solution(mesh):
    return jax.shard_map(
        functools.partial(local, dict(mesh.shape)),
        mesh=mesh,
        in_specs=(
            P(None, "row", "col"),
            P(),
            P("row", "col", None, None, None),
            P("row", "col", None, None),
            P("row", "col", None),
        ),
        out_specs=(P(None, "row", "col"), P()),
        check_vma=False,
    )
```

profile of v0, /device:TPU:0, one launch (start us, length us, event | category | flops | bytes accessed | tf_op | source)
XLA Modules:
  0.0 82.0 jit_solution(13097948228976141720)
XLA Ops:
  0.6 77.5 %shard_map.104 = (f32[2,512,512]{2,1,0:T(8,128)}, f32[2,256,256]{2,1,0:T(8,128)}) custom-call(s32[2,2]{1,0:T(2,128)} %bitcast.4, s32[2]{0:T(128)} %bitcast.5, f32[2,512,512]{2,1,0:T(8,128)} %obj.1, f32[2,256,256]{2,1,0:T(8,128)} %probe_in.1, f32[2,256,256]{2,1,0:T(8,128)} %bitcast.3, bf16[512,256]{1,0:T(8,128)(2,1)} %constant.8.clone.lh_in, ...), custom_call_target="tpu_custom_call" | custom-call | tf_op jit(solution)/shard_map/pallas_call | solution.py:607
  78.1 0.0 copy-start
  78.1 3.1 %copy.13 = f32[2,512,512]{2,1,0:T(8,128)} copy(f32[2,512,512]{2,1,0:T(8,128)} %get-tuple-element.4) | data formatting | bytes 4194304
  81.2 0.0 copy-done
  81.3 0.8 copy.14
Async XLA Ops:
  78.1 3.1 %copy-start = (f32[2,256,256]{2,1,0:T(8,128)S(1)}, f32[2,256,256]{2,1,0:T(8,128)}, u32[]{:S(2)}) copy-start(f32[2,256,256]{2,1,0:T(8,128)} %get-tuple-element.5) | copy-start | bytes 1572868
where the time goes:
time: 82.3 us; the launch traced here: 82 us
  Pallas kernels  77.5 us (94%)
  local copies, waits for them, and re-layouts  3.93 us (5%)
    pallas_call x1, Pallas kernels, local(): pl.pallas_call(functools.partial(kernel, rows, cols), out_shape=(jax.Shap...  77.5 us
    unnamed x4, local copies, waits for them, and re-layouts  3.93 us

commit v1 on v0

--- a/solution.py
+++ b/solution.py
@@ -17,7 +17,8 @@
 EPSILON = 1e-06
 
 UP, DOWN, LEFT, RIGHT = 0, 1, 2, 3
-CHUNKS = 4
+CHUNKS = 8
+SPLITS = 2
 
 
 def dft_tables(size_w):
@@ -102,9 +103,9 @@
 
 def kernel(
     rows, cols, pos, order, obj, probe_in, amps_in, lh_in, lr_in, rh_in, rr_in,
-    out, probe_out,
+    change_out, probe_out,
     own, rim, mid, probe, amps, lh, lr, rh, rr, info, infos, hs, hr, vbuf, placed,
-    bs, br, bnd_s, bnd_r, dreg, cs, cr, mid_s, mid_r, rim_s, rim_r,
+    bs, br, bnd_s, bnd_r, dreg, cs, cr, xs, xr, ws, wr, body_s, body_r, turn_s, turn_r,
     psum, acc, rx0, rx1, red, rx2, res, pw, pw0, pwa, pw1, pw2,
     local_sems, send_sems, recv_sems,
 ):
@@ -146,14 +147,6 @@
     sent = []
     lanes = [pl.ds(block * OV, OV) for block in range(blocks)]
     own_in = [fetch(obj.at[:, :, lanes[block]], own.at[:, block]) for block in range(blocks)]
-    rim_in = [
-        fetch(obj.at[:, :, lanes[block]], rim.at[side, :, pl.ds(OV, tile), :])
-        for side, block in ((0, 0), (1, blocks - 1))
-    ]
-    tall_in = [
-        fetch(obj.at[:, :, lanes[block]], mid.at[block - 1, :, pl.ds(OV, tile), :])
-        for block in range(1, blocks - 1)
-    ]
     rest_in = [
         fetch(source, target)
         for source, target in (
@@ -225,17 +218,20 @@
             hs.at[side, 0], hr.at[1 - side, 0], (west, east)[side]
         )
 
+    for side in range(2):
+        for part in range(2):
+            rim[side, part, pl.ds(OV, tile), :] = own[part, side_block[side]]
     squares = jnp.zeros((8, OV), jnp.float32)
     for part in range(2):
         for block in range(blocks):
             value = own[part, block]
+            if 0 < block < blocks - 1:
+                mid[block - 1, part, pl.ds(OV, tile), :] = value
             squares = squares + jnp.sum((value * value).reshape(tile // 8, 8, OV), axis=0)
     pw[...] = squares
 
     for copy in edge_in:
         copy.wait_recv()
-    for copy in rim_in:
-        copy.wait()
     for side in range(2):
         spot = wanted[side]
         start = jnp.where(spot.up == 1, spot.row + OV, spot.row + 2 * OV)
@@ -247,8 +243,6 @@
 
     for copy in mid_in:
         copy.wait_recv()
-    for copy in tall_in:
-        copy.wait()
     for copy in rest_in:
         copy.wait()
     spots(UP)
@@ -314,11 +308,11 @@
         rows_of = pl.ds(start, count)
         return across(*[placed[index, block, rows_of, :] for block in range(span // OV)])
 
-    def frame(batch, part, kind):
+    def frame(batch, part, kind, low=0, count=OV):
         spot = mine[batch]
         upper, lower = {"past": (-OV, tile), "edge": (0, tile - OV), "deep": (OV, half)}[kind]
         start = OV - spot.row + jnp.where(spot.up == 1, upper, lower)
-        return load_placed(2 * batch + part, start, OV)
+        return load_placed(2 * batch + part, start + low, count)
 
     transform(0)
 
@@ -328,52 +322,57 @@
     spot = mine[0]
     for chunk in range(CHUNKS):
         kind = ("edge", "deep")[chunk // per]
+        if chunk % per == 0:
+            values = [frame(0, part, kind) for part in range(2)]
+            values = [pick(spot.left, v[:, : 2 * OV], v[:, span - 2 * OV :]) for v in values]
         low = (chunk % per) * split
         for part in range(2):
-            value = frame(0, part, kind)[low : low + split]
-            bs[chunk, part] = pick(spot.left, value[:, : 2 * OV], value[:, span - 2 * OV :])
+            bs[chunk, part] = values[part][low : low + split]
         block_in.append(send(bs.at[chunk], br.at[par, chunk], partner))
-
-    def hand_on(copy, buffer, index):
-        copy.wait_recv()
-        return send(buffer.at[1 - par, index], buffer.at[par, index], onward)
-
     for part in range(2):
         value = frame(0, part, "past")
-        cs[0, part] = pick(spot.left, value[:, :OV], value[:, span - OV :])
-    for chunk in range(per):
-        block_on.append(hand_on(block_in[chunk], br, chunk))
-    corner_in = [send(cs.at[0], cr.at[par, 0], partner)]
-    for copy in block_on:
-        copy.wait_recv()
+        cs[part] = pick(spot.left, value[:, :OV], value[:, span - OV :])
+    corner_in = send(cs, cr.at[par], partner)
+
+    def hand_on(copy, buffer, *index):
+        copy.wait_recv()
+        return send(buffer.at[(1 - par,) + index], buffer.at[(par,) + index], onward)
 
     def near_block(side, part, kind):
         base = 0 if kind == "edge" else per
         return stacked(*[br[side, base + k, part] for k in range(per)])
 
     toward = (1 - near[LEFT][0].left, near[RIGHT][0].left)
-    blank = jnp.zeros((OV, span - 2 * OV), jnp.float32)
+    blank = jnp.zeros((split, span - 2 * OV), jnp.float32)
     band_in = []
-    for way, slot in ((0, UP), (1, DOWN)):
-        goal = near[slot][1]
-        match = spot.up if way == 0 else 1 - spot.up
-        use_own = match * same(spot.left, goal.left)
-        ups = [near[LEFT][0].up, near[RIGHT][0].up]
-        if way == 1:
-            ups = [1 - flag for flag in ups]
-        use = jnp.where(goal.left == 1, ups[0] * toward[0], ups[1] * toward[1])
-        for part in range(2):
-            block = pick(goal.left, near_block(0, part, "edge"), near_block(1, part, "edge"))
-            block = keep(use, block)
-            whole = keep(use_own, frame(0, part, "edge"))
-            whole = whole + pick(goal.left, across(block, blank), across(blank, block))
-            bnd_s[way, part] = cut(whole, goal)
-        band_in.append(
-            send(bnd_s.at[way], bnd_r.at[1 - way], (above, below)[way])
-        )
-    for chunk in range(per, CHUNKS):
+
+    def send_bands(chunk):
+        for way, slot in ((0, UP), (1, DOWN)):
+            goal = near[slot][1]
+            match = spot.up if way == 0 else 1 - spot.up
+            use_own = match * same(spot.left, goal.left)
+            ups = [near[LEFT][0].up, near[RIGHT][0].up]
+            if way == 1:
+                ups = [1 - flag for flag in ups]
+            use = jnp.where(goal.left == 1, ups[0] * toward[0], ups[1] * toward[1])
+            for part in range(2):
+                block = keep(use, pick(goal.left, br[0, chunk, part], br[1, chunk, part]))
+                whole = keep(use_own, frame(0, part, "edge", chunk * split, split))
+                whole = whole + pick(goal.left, across(block, blank), across(blank, block))
+                bnd_s[way, chunk, part] = cut(whole, goal)
+            band_in.append(
+                send(bnd_s.at[way, chunk], bnd_r.at[1 - way, chunk], (above, below)[way])
+            )
+
+    lead = min(3, per)
+    for chunk in range(lead):
         block_on.append(hand_on(block_in[chunk], br, chunk))
-    corner_on = [hand_on(corner_in[0], cr, 0)]
+    for chunk in range(per):
+        block_on[chunk].wait_recv()
+        send_bands(chunk)
+        block_on.append(hand_on(block_in[chunk + lead], br, chunk + lead))
+    for chunk in range(per + lead, CHUNKS):
+        block_on.append(hand_on(block_in[chunk], br, chunk))
     for copy in block_on[per:]:
         copy.wait_recv()
 
@@ -393,7 +392,8 @@
     for copy in band_in:
         copy.wait_recv()
     for part in range(2):
-        band = pick(spot.up, bnd_r[0, part], bnd_r[1, part])
+        bands = [pick(spot.up, bnd_r[0, k, part], bnd_r[1, k, part]) for k in range(per)]
+        band = stacked(*bands)
         region = pick(spot.up, stacked(band, inside[part]), stacked(inside[part], band))
         for block in range(size_w // OV):
             dreg[part, block] = region[:, block * OV : (block + 1) * OV]
@@ -405,25 +405,6 @@
 
     pair_in = send(psum.at[1 - core], rx0, sibling)
     power_in = [send(pw, pw0, sibling)]
-
-    for index, kind in ((1, "past"), (2, "edge"), (3, "deep")):
-        for part in range(2):
-            value = frame(1, part, kind)
-            cs[index, part] = pick(spot.left, value[:, :OV], value[:, span - OV :])
-    pair_in.wait_recv()
-    acc[...] = psum[core] + rx0[...]
-    power_in[0].wait_recv()
-    pwa[...] = pw[...] + pw0[...]
-    piece = size_w // cols
-    part_in = []
-    for step in range(1, cols):
-        other = (col + step) % cols
-        part_in.append(
-            send(acc.at[pl.ds(other * piece, piece)], rx1.at[step - 1], at(row, other))
-        )
-        power_in.append(send(pwa, pw1.at[col], at(row, other)))
-    for index in range(1, 4):
-        corner_in.append(send(cs.at[index], cr.at[par, index], partner))
 
     first_up = mine[0].up
     out_spots = (
@@ -433,28 +414,63 @@
     out_batch = (1 - first_up, first_up)
     up_start = jnp.maximum(OV - out_spots[0].row, OV)
 
-    def wide_own(way, part, start, count):
+    def own_half(way, part, start, count):
         value = load_placed(2 * out_batch[way] + part, start, count)
-        left = out_spots[way].left
-        body = pick(left, value[:, OV:], value[:, :half])
-        gap = jnp.zeros((count, half), jnp.float32)
-        return pick(left, across(body, gap), across(gap, body))
+        return pick(out_spots[way].left, value[:, OV:], value[:, :half])
 
     past_in = []
     for way in range(2):
         start = up_start - OV if way == 0 else OV + tile - out_spots[1].row
         for part in range(2):
-            value = wide_own(way, part, start, OV)
-            mid_s[way, part] = value[:, OV : tile - OV]
-            rim_s[way, 0, part] = value[:, :OV]
-            rim_s[way, 1, part] = value[:, tile - OV :]
-
-    mine_piece = acc[pl.ds(pl.multiple_of(col * piece, piece), piece), :]
-    for copy in part_in:
-        copy.wait_recv()
-    for step in range(cols - 1):
-        mine_piece = mine_piece + rx1[step]
-    red[...] = mine_piece
+            body_s[way, part] = own_half(way, part, start, OV)
+        past_in.append(send(body_s.at[way], body_r.at[1 - way], (above, below)[way]))
+    spot = mine[1]
+
+    def outer(part, kind, low=0, count=OV):
+        value = frame(1, part, kind, low, count)
+        return pick(spot.left, value[:, :OV], value[:, span - OV :])
+
+    for part in range(2):
+        for chunk in range(per):
+            xs[chunk, part] = outer(part, "past", chunk * split, split)
+        for index, kind in enumerate(("edge", "deep")):
+            ws[index, part] = outer(part, kind)
+
+    pair_in.wait_recv()
+    acc[...] = psum[core] + rx0[...]
+    power_in[0].wait_recv()
+    pwa[...] = pw[...] + pw0[...]
+    piece = size_w // cols
+    sub = piece // SPLITS
+
+    def slab(place, part):
+        return pl.ds(pl.multiple_of(place * piece + part * sub, sub), sub)
+
+    part_in = [[] for _ in range(SPLITS)]
+    for half_of in range(SPLITS):
+        for step in range(1, cols):
+            other = (col + step) % cols
+            part_in[half_of].append(
+                send(acc.at[slab(other, half_of)], rx1.at[step - 1, half_of], at(row, other))
+            )
+            if half_of == 0:
+                power_in.append(send(pwa, pw1.at[col], at(row, other)))
+    corner_on = [hand_on(corner_in, cr)]
+    turn_from = [send(xs.at[k], xr.at[par, k], partner) for k in range(per)]
+    strip_in = [send(ws.at[k], wr.at[par, k], partner) for k in range(2)]
+
+    plane = row // 2
+    plane_in = [[] for _ in range(SPLITS)]
+    for half_of in range(SPLITS):
+        mine_piece = acc[slab(col, half_of), :]
+        for copy in part_in[half_of]:
+            copy.wait_recv()
+        for step in range(cols - 1):
+            mine_piece = mine_piece + rx1[step, half_of]
+        red[half_of] = mine_piece
+        for step in range(1, rows // 2):
+            goal = at((row + 2 * step) % rows, col)
+            plane_in[half_of].append(send(red.at[half_of], rx2.at[plane, half_of], goal))
     for copy in power_in[1:]:
         copy.wait_recv()
     pw1[col] = pwa[...]
@@ -462,88 +478,99 @@
     for place in range(1, cols):
         total = total + pw1[place]
     pw2[rows // 2] = total
-    plane = row // 2
-    plane_in = []
     for step in range(1, rows // 2):
         goal = at((row + 2 * step) % rows, col)
-        plane_in.append(send(red, rx2.at[plane], goal))
-        plane_in.append(send(pw2.at[rows // 2], pw2.at[plane], goal))
-    for way in range(2):
-        past_in.append(send(mid_s.at[way], mid_r.at[1 - way], (above, below)[way]))
-
-    corner_on.append(hand_on(corner_in[1], cr, 1))
-    corner_on.append(hand_on(corner_in[2], cr, 2))
-    corner_on.append(hand_on(corner_in[3], cr, 3))
-
-    for copy in plane_in:
-        copy.wait_recv()
-    rx2[plane] = red[...]
-    pw2[plane] = total
-    whole, total = rx2[0], pw2[0]
-    for place in range(1, rows // 2):
-        whole = whole + rx2[place]
-        total = total + pw2[place]
-    here = pl.ds(pl.multiple_of(col * piece, piece), piece)
-    res[core, here, :] = whole
-    gather_in = []
-    for step in range(1, cols):
-        other = at(row, (col + step) % cols)
-        gather_in.append(send(res.at[core, here], res.at[core, here], other))
-
-    corner_on[0].wait_recv()
-    corner_on[1].wait_recv()
+        plane_in[1].append(send(pw2.at[rows // 2], pw2.at[plane], goal))
+    for chunk in range(per):
+        corner_on.append(hand_on(turn_from[chunk], xr, chunk))
+    for copy in corner_on:
+        copy.wait_recv()
+    turn_in = []
     for way in range(2):
         for side in range(2):
-            theirs = wanted[side]
-            first = (west_first, east_first)[side]
+            theirs, first = wanted[side], (west_first, east_first)[side]
             match = theirs.up if way == 0 else 1 - theirs.up
             for part in range(2):
-                corner = pick(first, cr[side, 0, part], cr[side, 1, part])
-                rim_s[way, side, part] = rim_s[way, side, part] + keep(match, corner)
-    for way in range(2):
-        past_in.append(send(rim_s.at[way], rim_r.at[1 - way], (above, below)[way]))
-
-    for copy in gather_in:
-        copy.wait_recv()
-    last_in = send(res.at[core], res.at[core], sibling)
-
-    corner_on[2].wait_recv()
-    corner_on[3].wait_recv()
-    for copy in past_in:
+                fresh = stacked(*[xr[side, k, part] for k in range(per)])
+                turn_s[way, side, part] = keep(match, pick(first, cr[side, part], fresh))
+        turn_in.append(send(turn_s.at[way], turn_r.at[1 - way], (above, below)[way]))
+
+    strip_on = []
+    gather_in, last_in = [[] for _ in range(SPLITS)], []
+    for half_of in range(SPLITS):
+        for copy in plane_in[half_of]:
+            copy.wait_recv()
+        rx2[plane, half_of] = red[half_of]
+        whole = rx2[0, half_of]
+        for place in range(1, rows // 2):
+            whole = whole + rx2[place, half_of]
+        here = slab(col, half_of)
+        res[core, here, :] = whole
+        for step in range(1, cols):
+            other = at(row, (col + step) % cols)
+            gather_in[half_of].append(send(res.at[core, here], res.at[core, here], other))
+        last_in.append(send(res.at[core, here], res.at[core, here], sibling))
+        strip_on.append(hand_on(strip_in[half_of], wr, half_of))
+    pw2[plane] = total
+    total = pw2[0]
+    for place in range(1, rows // 2):
+        total = total + pw2[place]
+
+    for half_of in range(SPLITS):
+        for step, copy in enumerate(gather_in[half_of]):
+            copy.wait_recv()
+            came = slab((col + cols - 1 - step) % cols, half_of)
+            last_in.append(send(res.at[core, came], res.at[core, came], sibling))
+
+    for copy in strip_on:
         copy.wait_recv()
     gap = jnp.zeros((half, tile - 2 * OV), jnp.float32)
-    for part in range(2):
-        outer = []
+    changes = []
+    for part in range(2):
+        strips_of = []
         for side in range(2):
-            first = (west_first, east_first)[side]
+            theirs, first = wanted[side], (west_first, east_first)[side]
             part_of = slice(OV, 2 * OV) if side == 0 else slice(0, OV)
-            at_edge = pick(first, near_block(side, part, "edge")[:, part_of], cr[side, 2, part])
-            deep = pick(first, near_block(side, part, "deep")[:, part_of], cr[side, 3, part])
-            up = wanted[side].up
-            outer.append((up, at_edge, deep))
+            at_edge = near_block(side, part, "edge")[:, part_of]
+            deep = near_block(side, part, "deep")[:, part_of]
+            early = pick(theirs.up, stacked(at_edge, deep), stacked(deep, at_edge))
+            fresh = pick(
+                theirs.up,
+                stacked(wr[side, 0, part], wr[side, 1, part]),
+                stacked(wr[side, 1, part], wr[side, 0, part]),
+            )
+            strips_of.append((theirs.up, pick(first, early, fresh)))
         for way in range(2):
             start = up_start if way == 0 else OV + half - out_spots[1].row
-            value = wide_own(way, part, start, half)
-            strips = []
-            for up, at_edge, deep in outer:
-                flag = up if way == 0 else 1 - up
-                strips.append(
-                    keep(flag, stacked(at_edge, deep) if way == 0 else stacked(deep, at_edge))
-                )
-            value = value + across(strips[0], gap, strips[1])
-            late = across(rim_r[way, 0, part], mid_r[way, part], rim_r[way, 1, part])
-            rest = jnp.zeros((half - OV, tile), jnp.float32)
-            value = value + (stacked(late, rest) if way == 0 else stacked(rest, late))
-            band = pl.ds(way * half, half)
-            old = across(*[own[part, block, band, :] for block in range(blocks)])
-            out[part, band, :] = old - value
-
-    last_in.wait_recv()
+            body = own_half(way, part, start, half)
+            space = jnp.zeros((half, half), jnp.float32)
+            value = pick(out_spots[way].left, across(body, space), across(space, body))
+            strips = [keep(up if way == 0 else 1 - up, strip) for up, strip in strips_of]
+            changes.append(value + across(strips[0], gap, strips[1]))
+
+    for copy in past_in + turn_in:
+        copy.wait_recv()
+    gap = jnp.zeros((OV, tile - 2 * OV), jnp.float32)
+    space = jnp.zeros((OV, half), jnp.float32)
+    rest = jnp.zeros((half - OV, tile), jnp.float32)
+    for part in range(2):
+        for way in range(2):
+            spots_of = near[(UP, DOWN)[way]]
+            flag = 1 - spots_of[0].up if way == 0 else spots_of[0].up
+            left = jnp.where(flag == 1, spots_of[0].left, spots_of[1].left)
+            body = body_r[way, part]
+            late = pick(left, across(body, space), across(space, body))
+            late = late + across(turn_r[way, 0, part], gap, turn_r[way, 1, part])
+            late = stacked(late, rest) if way == 0 else stacked(rest, late)
+            change_out[part, pl.ds(way * half, half), :] = changes[2 * part + way] + late
+
+    for copy in last_in:
+        copy.wait_recv()
     cell_count = float(tile * tile * rows * cols)
     mean_power = jnp.sum(total, axis=(0, 1), keepdims=True) / cell_count + EPSILON
     step_probe = BETA * size_w * size_w / (cell_count * mean_power)
     for part in range(2):
-        probe_out[part] = probe[part] - step_probe * res[part]
+        probe_out[part] = step_probe * res[part]
     for copy in sent:
         copy.wait_send()
 
@@ -577,21 +604,25 @@
         placed=f32(4, span // OV, size_w + 2 * OV, OV),
         bs=f32(CHUNKS, 2, split, 2 * OV),
         br=f32(2, CHUNKS, 2, split, 2 * OV),
-        bnd_s=f32(2, 2, OV, size_w),
-        bnd_r=f32(2, 2, OV, size_w),
+        bnd_s=f32(2, OV // split, 2, split, size_w),
+        bnd_r=f32(2, OV // split, 2, split, size_w),
         dreg=f32(2, size_w // OV, span, OV),
-        cs=f32(4, 2, OV, OV),
-        cr=f32(2, 4, 2, OV, OV),
-        mid_s=f32(2, 2, OV, tile - 2 * OV),
-        mid_r=f32(2, 2, OV, tile - 2 * OV),
-        rim_s=f32(2, 2, 2, OV, OV),
-        rim_r=f32(2, 2, 2, OV, OV),
+        cs=f32(2, OV, OV),
+        cr=f32(2, 2, OV, OV),
+        xs=f32(OV // split, 2, split, OV),
+        xr=f32(2, OV // split, 2, split, OV),
+        ws=f32(2, 2, OV, OV),
+        wr=f32(2, 2, 2, OV, OV),
+        body_s=f32(2, 2, OV, half),
+        body_r=f32(2, 2, OV, half),
+        turn_s=f32(2, 2, 2, OV, OV),
+        turn_r=f32(2, 2, 2, OV, OV),
         psum=f32(2, size_w, size_w),
         acc=f32(size_w, size_w),
         rx0=f32(size_w, size_w),
-        rx1=f32(cols - 1, piece, size_w),
-        red=f32(piece, size_w),
-        rx2=f32(rows // 2, piece, size_w),
+        rx1=f32(cols - 1, SPLITS, piece // SPLITS, size_w),
+        red=f32(SPLITS, piece // SPLITS, size_w),
+        rx2=f32(rows // 2, SPLITS, piece // SPLITS, size_w),
         res=f32(2, size_w, size_w),
         pw=f32(8, 128),
         pw0=f32(8, 128),
@@ -600,11 +631,12 @@
         pw2=f32(rows // 2 + 1, 8, 128),
     )
     sends = 96 + 4 * cols + 2 * rows
-    hbm = pl.BlockSpec(memory_space=pl.ANY)
+    hbm = pl.BlockSpec(memory_space=pltpu.HBM)
     vmem = pl.BlockSpec(memory_space=pltpu.VMEM)
     smem = pl.BlockSpec(memory_space=pltpu.SMEM)
     dma = pltpu.SemaphoreType.DMA
-    return pl.pallas_call(
+    fixed = lambda value: pltpu.with_memory_space_constraint(value, pltpu.HBM)
+    change, probe_change = pl.pallas_call(
         functools.partial(kernel, rows, cols),
         out_shape=(
             jax.ShapeDtypeStruct(object_field.shape, jnp.float32),
@@ -614,19 +646,20 @@
         out_specs=(vmem, vmem),
         scratch_shapes=list(scratch.values()) + [dma((32,)), dma((sends,)), dma((sends,))],
         compiler_params=pltpu.CompilerParams(
-            collective_id=0, has_side_effects=True, vmem_limit_bytes=56 * 1024 * 1024
+            collective_id=0, has_side_effects=True, vmem_limit_bytes=36 * 1024 * 1024
         ),
     )(
-        positions[0, 0],
-        batch_order[0, 0],
-        object_field,
-        probe_field,
-        amplitudes[0, 0],
-        jnp.asarray(np.concatenate(np.split(head, 2, axis=1), axis=0)),
-        jnp.asarray(np.concatenate(np.split(rest, 2, axis=1), axis=0)),
-        jnp.asarray(head),
-        jnp.asarray(rest),
+        fixed(positions[0, 0]),
+        fixed(batch_order[0, 0]),
+        fixed(object_field),
+        fixed(probe_field),
+        fixed(amplitudes[0, 0]),
+        fixed(jnp.asarray(np.concatenate(np.split(head, 2, axis=1), axis=0))),
+        fixed(jnp.asarray(np.concatenate(np.split(rest, 2, axis=1), axis=0))),
+        fixed(jnp.asarray(head)),
+        fixed(jnp.asarray(rest)),
     )
+    return object_field - change, probe_field - probe_change
 
 
 def solution(mesh):

time: 82.3 us -> 75.4 us (0.916)
  Pallas kernels: 77.5 us -> 72 us
  local copies, waits for them, and re-layouts: 3.93 us -> 0.01 us
  other arithmetic: 0 us -> 2.66 us
    pallas_call x1, Pallas kernels: 77.5 us -> 72 us  [local(): pl.pallas_call(functools.partial(kernel, rows, cols), out_shape=(jax.Shap...]
    unnamed x4, local copies, waits for them, and re-layouts: 3.93 us -> 0.01 us
    sub x0 -> x2, other arithmetic: none -> 2.66 us  [local(): return (object_field - change, probe_field - probe_change)]
where the time goes in v1:
time: 75.4 us; the launch traced here: 75.3 us
  Pallas kernels  72 us (95%)
  other arithmetic  2.66 us (4%)
    pallas_call x1, Pallas kernels, local(): pl.pallas_call(functools.partial(kernel, rows, cols), out_shape=(jax.Shap...  72 us
    sub x2, other arithmetic, local(): return (object_field - change, probe_field - probe_change)  2.66 us

profile of v1, /device:TPU:0, one launch (start us, length us, event | category | flops | bytes accessed | tf_op | source)
XLA Modules:
  0.0 75.3 jit_solution(6771327696024995070)
XLA Ops:
  0.6 0.0 copy-start
  0.6 72.0 %shard_map.104 = (f32[2,512,512]{2,1,0:T(8,128)S(1)}, f32[2,256,256]{2,1,0:T(8,128)S(1)}) custom-call(s32[2,2]{1,0:T(2,128)} %bitcast.4, s32[2]{0:T(128)} %bitcast.5, f32[2,512,512]{2,1,0:T(8,128)} %obj.1, f32[2,256,256]{2,1,0:T(8,128)} %probe_in.1, f32[2,256,256]{2,1,0:T(8,128)} %bitcast.3, bf16[512,256]{1,0:T(8,128)(2,1)} %constant.8.clone.lh_in, ...), custom_call_target="tpu_custom_call" | custom-call | tf_op jit(solution)/shard_map/pallas_call | solution.py:639
  72.7 0.0 copy-done
  72.7 0.0 copy-start.1
  72.7 1.8 %sub.6 = f32[2,512,512]{2,1,0:T(8,128)} subtract(f32[2,512,512]{2,1,0:T(8,128)S(1)} %copy-done, f32[2,512,512]{2,1,0:T(8,128)S(1)} %get-tuple-element.4) | non-fusion elementwise | flops 524288 | bytes 6291456 | tf_op jit(solution)/shard_map/sub | solution.py:662
  74.5 0.0 copy-done.1
  74.5 0.9 %sub.7 = f32[2,256,256]{2,1,0:T(8,128)} subtract(f32[2,256,256]{2,1,0:T(8,128)S(1)} %copy-done.1, f32[2,256,256]{2,1,0:T(8,128)S(1)} %get-tuple-element.5) | non-fusion elementwise | flops 131072 | bytes 1572864 | tf_op jit(solution)/shard_map/sub | solution.py:662
Async XLA Ops:
  0.6 72.0 %copy-start = (f32[2,512,512]{2,1,0:T(8,128)S(1)}, f32[2,512,512]{2,1,0:T(8,128)}, u32[]{:S(2)}) copy-start(f32[2,512,512]{2,1,0:T(8,128)} %obj.1) | copy-start | bytes 6291460
  72.7 1.8 %copy-start.1 = (f32[2,256,256]{2,1,0:T(8,128)S(1)}, f32[2,256,256]{2,1,0:T(8,128)}, u32[]{:S(2)}) copy-start(f32[2,256,256]{2,1,0:T(8,128)} %probe_in.1) | copy-start | bytes 1572868

commit v2 on v1

--- a/solution.py
+++ b/solution.py
@@ -406,36 +406,6 @@
     pair_in = send(psum.at[1 - core], rx0, sibling)
     power_in = [send(pw, pw0, sibling)]
 
-    first_up = mine[0].up
-    out_spots = (
-        choose(first_up, mine[0], mine[1], tile),
-        choose(first_up, mine[1], mine[0], tile),
-    )
-    out_batch = (1 - first_up, first_up)
-    up_start = jnp.maximum(OV - out_spots[0].row, OV)
-
-    def own_half(way, part, start, count):
-        value = load_placed(2 * out_batch[way] + part, start, count)
-        return pick(out_spots[way].left, value[:, OV:], value[:, :half])
-
-    past_in = []
-    for way in range(2):
-        start = up_start - OV if way == 0 else OV + tile - out_spots[1].row
-        for part in range(2):
-            body_s[way, part] = own_half(way, part, start, OV)
-        past_in.append(send(body_s.at[way], body_r.at[1 - way], (above, below)[way]))
-    spot = mine[1]
-
-    def outer(part, kind, low=0, count=OV):
-        value = frame(1, part, kind, low, count)
-        return pick(spot.left, value[:, :OV], value[:, span - OV :])
-
-    for part in range(2):
-        for chunk in range(per):
-            xs[chunk, part] = outer(part, "past", chunk * split, split)
-        for index, kind in enumerate(("edge", "deep")):
-            ws[index, part] = outer(part, kind)
-
     pair_in.wait_recv()
     acc[...] = psum[core] + rx0[...]
     power_in[0].wait_recv()
@@ -456,8 +426,39 @@
             if half_of == 0:
                 power_in.append(send(pwa, pw1.at[col], at(row, other)))
     corner_on = [hand_on(corner_in, cr)]
+
+    first_up = mine[0].up
+    out_spots = (
+        choose(first_up, mine[0], mine[1], tile),
+        choose(first_up, mine[1], mine[0], tile),
+    )
+    out_batch = (1 - first_up, first_up)
+    up_start = jnp.maximum(OV - out_spots[0].row, OV)
+
+    def own_half(way, part, start, count):
+        value = load_placed(2 * out_batch[way] + part, start, count)
+        return pick(out_spots[way].left, value[:, OV:], value[:, :half])
+
+    spot = mine[1]
+
+    def outer(part, kind, low=0, count=OV):
+        value = frame(1, part, kind, low, count)
+        return pick(spot.left, value[:, :OV], value[:, span - OV :])
+
+    for part in range(2):
+        for chunk in range(per):
+            xs[chunk, part] = outer(part, "past", chunk * split, split)
     turn_from = [send(xs.at[k], xr.at[par, k], partner) for k in range(per)]
+    for part in range(2):
+        for index, kind in enumerate(("edge", "deep")):
+            ws[index, part] = outer(part, kind)
     strip_in = [send(ws.at[k], wr.at[par, k], partner) for k in range(2)]
+    past_in = []
+    for way in range(2):
+        start = up_start - OV if way == 0 else OV + tile - out_spots[1].row
+        for part in range(2):
+            body_s[way, part] = own_half(way, part, start, OV)
+        past_in.append(send(body_s.at[way], body_r.at[1 - way], (above, below)[way]))
 
     plane = row // 2
     plane_in = [[] for _ in range(SPLITS)]
@@ -483,17 +484,19 @@
         plane_in[1].append(send(pw2.at[rows // 2], pw2.at[plane], goal))
     for chunk in range(per):
         corner_on.append(hand_on(turn_from[chunk], xr, chunk))
-    for copy in corner_on:
-        copy.wait_recv()
     turn_in = []
-    for way in range(2):
-        for side in range(2):
-            theirs, first = wanted[side], (west_first, east_first)[side]
-            match = theirs.up if way == 0 else 1 - theirs.up
-            for part in range(2):
-                fresh = stacked(*[xr[side, k, part] for k in range(per)])
-                turn_s[way, side, part] = keep(match, pick(first, cr[side, part], fresh))
-        turn_in.append(send(turn_s.at[way], turn_r.at[1 - way], (above, below)[way]))
+
+    def send_turns():
+        for copy in corner_on:
+            copy.wait_recv()
+        for way in range(2):
+            for side in range(2):
+                theirs, first = wanted[side], (west_first, east_first)[side]
+                match = theirs.up if way == 0 else 1 - theirs.up
+                for part in range(2):
+                    fresh = stacked(*[xr[side, k, part] for k in range(per)])
+                    turn_s[way, side, part] = keep(match, pick(first, cr[side, part], fresh))
+            turn_in.append(send(turn_s.at[way], turn_r.at[1 - way], (above, below)[way]))
 
     strip_on = []
     gather_in, last_in = [[] for _ in range(SPLITS)], []
@@ -510,6 +513,9 @@
             other = at(row, (col + step) % cols)
             gather_in[half_of].append(send(res.at[core, here], res.at[core, here], other))
         last_in.append(send(res.at[core, here], res.at[core, here], sibling))
+        if half_of == 0:
+            send_turns()
+    for half_of in range(2):
         strip_on.append(hand_on(strip_in[half_of], wr, half_of))
     pw2[plane] = total
     total = pw2[0]

time: 75.4 us -> 74.4 us (0.987)
  Pallas kernels: 72 us -> 70.9 us
    pallas_call x1, Pallas kernels: 72 us -> 70.9 us  [local(): pl.pallas_call(functools.partial(kernel, rows, cols), out_shape=(jax.Shap...]
where the time goes in v2:
time: 74.4 us; the launch traced here: 74.2 us
  Pallas kernels  70.9 us (95%)
  other arithmetic  2.66 us (4%)
    pallas_call x1, Pallas kernels, local(): pl.pallas_call(functools.partial(kernel, rows, cols), out_shape=(jax.Shap...  70.9 us
    sub x2, other arithmetic, local(): return (object_field - change, probe_field - probe_change)  2.66 us

profile of v2, /device:TPU:0, one launch (start us, length us, event | category | flops | bytes accessed | tf_op | source)
XLA Modules:
  0.0 74.2 jit_solution(10696604252237431962)
XLA Ops:
  0.6 0.0 copy-start
  0.6 70.9 %shard_map.104 = (f32[2,512,512]{2,1,0:T(8,128)S(1)}, f32[2,256,256]{2,1,0:T(8,128)S(1)}) custom-call(s32[2,2]{1,0:T(2,128)} %bitcast.4, s32[2]{0:T(128)} %bitcast.5, f32[2,512,512]{2,1,0:T(8,128)} %obj.1, f32[2,256,256]{2,1,0:T(8,128)} %probe_in.1, f32[2,256,256]{2,1,0:T(8,128)} %bitcast.3, bf16[512,256]{1,0:T(8,128)(2,1)} %constant.8.clone.lh_in, ...), custom_call_target="tpu_custom_call" | custom-call | tf_op jit(solution)/shard_map/pallas_call | solution.py:645
  71.5 0.0 copy-done
  71.5 0.0 copy-start.1
  71.5 1.8 %sub.6 = f32[2,512,512]{2,1,0:T(8,128)} subtract(f32[2,512,512]{2,1,0:T(8,128)S(1)} %copy-done, f32[2,512,512]{2,1,0:T(8,128)S(1)} %get-tuple-element.4) | non-fusion elementwise | flops 524288 | bytes 6291456 | tf_op jit(solution)/shard_map/sub | solution.py:668
  73.4 0.0 copy-done.1
  73.4 0.9 %sub.7 = f32[2,256,256]{2,1,0:T(8,128)} subtract(f32[2,256,256]{2,1,0:T(8,128)S(1)} %copy-done.1, f32[2,256,256]{2,1,0:T(8,128)S(1)} %get-tuple-element.5) | non-fusion elementwise | flops 131072 | bytes 1572864 | tf_op jit(solution)/shard_map/sub | solution.py:668
Async XLA Ops:
  0.6 70.9 %copy-start = (f32[2,512,512]{2,1,0:T(8,128)S(1)}, f32[2,512,512]{2,1,0:T(8,128)}, u32[]{:S(2)}) copy-start(f32[2,512,512]{2,1,0:T(8,128)} %obj.1) | copy-start | bytes 6291460
  71.5 1.8 %copy-start.1 = (f32[2,256,256]{2,1,0:T(8,128)S(1)}, f32[2,256,256]{2,1,0:T(8,128)}, u32[]{:S(2)}) copy-start(f32[2,256,256]{2,1,0:T(8,128)} %probe_in.1) | copy-start | bytes 1572868
